TPU v7x, 32 devices: a whole 2x2x4 slice. The times are simulated.
32 devices in a mesh: gx: 8 (over y, x, core), gy: 4 (over z).
Axes of the slice: x: 2, y: 2, z: 4, core: 2. Of those that a mesh axis runs over, the one named last changes fastest.
Arguments:
- cells: int32 [3, 1048576], P(None, ('gx', 'gy')), may hold values from 0 to 255, as said below
- fractions: float32 [3, 1048576], P(None, ('gx', 'gy')), may hold values from 0 to 1
- charges: float32 [1048576], P(('gx', 'gy')), may hold values from -24 to 24
- influence: float32 [256, 256, 256], P('gx', 'gy'), may hold values from 0.05 to 24, as said below
- shells: int32 [256, 256, 256], P('gx', 'gy'), may hold values from 0 to 255
Outputs:
- potential_hat: float32 [2, 256, 256, 256], P(None, 'gx', 'gy')
- energy: float32 [], replicated
- virial: float32 [3, 3], replicated
- spectrum: float32 [256], replicated
Inputs may be any that keep to these rules, and one draw needn't show every extreme that they name: `cells`: atom a belongs to device a // 32768, devices numbered with gy fastest; its y cell lies in that device's block of 32 y planes (block index its gx index) and its z cell in its block of 64 z planes (block index its gy index). `influence`: Positive.
All inputs are finite; a program needn't handle non-finite values.
Results may differ from a plain program's by a relative error of at most 0.0029.
Values sent between devices are 32-bit elements; how exact they have to be, the bound alone decides.
No kernel may reach another device: no remote copies, remote signals or barrier semaphores. Data moves between devices by JAX's collectives and lax.ppermute only.
A program may use at most 64 MiB of HBM per device.

v0:
```python
import math
import jax
import jax.numpy as jnp
from jax import lax
from jax.sharding import PartitionSpec as P

MESH = 256
SHELLS = 256
SCREEN = 4096


def passed_along(block, axis, distance):
    devices = range(lax.axis_size(axis))
    route = [((i - distance) % len(devices), i) for i in devices]
    return lax.ppermute(block, axis, route)


def spline(frac):
    cube = frac * frac * frac
    square = frac * frac
    rest = 1.0 - frac
    return (
        rest * rest * rest / 6.0,
        (3.0 * cube - 6.0 * square + 4.0) / 6.0,
        (-3.0 * cube + 3.0 * square + 3.0 * frac + 1.0) / 6.0,
        cube / 6.0,
    )


def place_weights(weights, target, columns, wrapped):
    result = jnp.zeros(columns.shape, jnp.float32)
    for offset in range(4):
        column = target[:, None] + offset
        if wrapped:
            column = column % MESH
        result = result + jnp.where(columns == column, weights[offset][:, None], 0.0)
    return result


def wave_tables():
    index = jnp.arange(MESH, dtype=jnp.int32)
    phase = index[:, None] * index[None, :] % MESH
    angle = phase.astype(jnp.float32) * (2.0 * math.pi / MESH)
    factor = 1.0 / math.sqrt(MESH)
    return (jnp.cos(angle) * factor, -jnp.sin(angle) * factor)


def wave_numbers(index):
    return jnp.where(index < MESH // 2, index, index - MESH).astype(jnp.float32)


def shards(cells, fractions, charges, influence, shells):
    rows_y = lax.axis_size("gx")
    cols_z = lax.axis_size("gy")
    plane_y = MESH // rows_y
    plane_z = MESH // cols_z
    first_y = lax.axis_index("gx") * plane_y
    first_z = lax.axis_index("gy") * plane_z
    ext_y = plane_y + 3
    ext_z = plane_z + 3
    count = charges.shape[0]
    block = min(2048, count)
    columns_x = lax.broadcasted_iota(jnp.int32, (block, MESH), 1)
    columns_y = lax.broadcasted_iota(jnp.int32, (block, ext_y), 1)
    columns_z = lax.broadcasted_iota(jnp.int32, (block, ext_z), 1)

    def spread(turn, accum):
        begin = turn * block
        cell = lax.dynamic_slice_in_dim(cells, begin, block, 1)
        frac = lax.dynamic_slice_in_dim(fractions, begin, block, 1)
        charge = lax.dynamic_slice_in_dim(charges, begin, block, 0)
        table_x = place_weights(spline(frac[0]), cell[0], columns_x, True)
        table_y = place_weights(spline(frac[1]), cell[1] - first_y, columns_y, False)
        wave_table_z = place_weights(spline(frac[2]), cell[2] - first_z, columns_z, False)
        factor_x = (charge[:, None] * table_x).astype(jnp.bfloat16)
        factor_yz = (
            (table_y[:, :, None] * wave_table_z[:, None, :])
            .reshape(block, ext_y * ext_z)
            .astype(jnp.bfloat16)
        )
        return accum + jnp.einsum(
            "ap,ax->px", factor_yz, factor_x, preferred_element_type=jnp.float32
        )

    spread_mesh = lax.fori_loop(
        0, count // block, spread, jnp.zeros((ext_y * ext_z, MESH), jnp.float32)
    )
    spread_mesh = spread_mesh.reshape(ext_y, ext_z, MESH)
    arrived = passed_along(spread_mesh[plane_y:], "gx", 1)
    spread_mesh = spread_mesh[:plane_y].at[:3].add(arrived)
    arrived_z = passed_along(spread_mesh[:, plane_z:], "gy", 1)
    spread_mesh = spread_mesh[:, :plane_z].at[:, :3].add(arrived_z)
    keep_y, keep_z = (plane_y, plane_z)
    cosine, minus_sine = wave_tables()
    real_table = jnp.stack([cosine, minus_sine])
    complex_table = jnp.stack([jnp.stack([cosine, -minus_sine]), jnp.stack([minus_sine, cosine])])
    upper_limit = lax.Precision.HIGHEST
    kx_rows = MESH // rows_y
    ky_rows = MESH // cols_z
    flat_mesh = spread_mesh.reshape(keep_y * keep_z, MESH)
    along_x = jnp.einsum("ckx,px->ckp", real_table, flat_mesh, precision=upper_limit)
    moved = lax.all_to_all(along_x[None], "gx", split_axis=2, concat_axis=0, tiled=True)
    moved = moved.reshape(rows_y, 2, kx_rows, keep_y, keep_z)
    table_y = complex_table.reshape(2, 2, MESH, rows_y, plane_y)
    along_y = jnp.einsum("ocKst,scktz->okKz", table_y, moved, precision=upper_limit)
    shifted_along_z = lax.all_to_all(
        along_y.reshape(2, kx_rows, MESH * keep_z)[None],
        "gy",
        split_axis=3,
        concat_axis=0,
        tiled=True,
    )
    shifted_along_z = shifted_along_z.reshape(cols_z, 2, kx_rows, ky_rows, keep_z)
    wave_table_z = complex_table.reshape(2, 2, MESH, cols_z, plane_z)
    structure_factor = jnp.einsum(
        "whzir,ihnqr->wnqz", wave_table_z, shifted_along_z, precision=upper_limit
    )
    wave_x = wave_numbers(lax.axis_index("gx") * kx_rows + jnp.arange(kx_rows, dtype=jnp.int32))[
        :, None, None
    ]
    wave_y = wave_numbers(lax.axis_index("gy") * ky_rows + jnp.arange(ky_rows, dtype=jnp.int32))[
        None, :, None
    ]
    wave_z = wave_numbers(jnp.arange(MESH, dtype=jnp.int32))[None, None, :]
    squared = wave_x * wave_x + wave_y * wave_y + wave_z * wave_z
    keep = jnp.where(squared > 0.0, 1.0, 0.0).astype(jnp.float32)
    weight = keep * influence
    potential_hat = structure_factor * weight[None]
    power = structure_factor[0] * structure_factor[0] + structure_factor[1] * structure_factor[1]
    influence_weighted = weight * power
    scale = 0.5 / MESH**3
    local_sum = jnp.sum(influence_weighted)
    coef = influence_weighted * 2.0 * (1.0 + squared / SCREEN) / (squared + 1.0 - keep)
    shape = coef.shape
    vectors = jnp.stack(
        [
            jnp.broadcast_to(wave_x, shape),
            jnp.broadcast_to(wave_y, shape),
            jnp.broadcast_to(wave_z, shape),
        ]
    )
    cross = jnp.einsum("akyz,bkyz->ab", vectors * coef[None], vectors, precision=upper_limit)
    virial_part = scale * (jnp.eye(3, dtype=jnp.float32) * local_sum - cross)
    energy_part = scale * local_sum
    shell_labels = jnp.arange(SHELLS, dtype=jnp.int32)

    def shell_rows(accum, pair):
        power_spectrum_row, shell_row = pair
        onehot = (shell_row.reshape(-1)[:, None] == shell_labels[None, :]).astype(jnp.float32)
        return (
            accum + jnp.dot(power_spectrum_row.reshape(-1), onehot, precision=upper_limit),
            None,
        )

    shell_sums, unused = lax.scan(shell_rows, jnp.zeros((SHELLS,), jnp.float32), (power, shells))
    spectrum_part = shell_sums * (SHELLS / MESH**3)
    energy, virial, spectrum = lax.psum((energy_part, virial_part, spectrum_part), ("gx", "gy"))
    return (potential_hat, energy, virial, spectrum)


def solution(mesh):
    return jax.shard_map(
        shards,
        mesh=mesh,
        in_specs=(
            P(None, ("gx", "gy")),
            P(None, ("gx", "gy")),
            P(("gx", "gy")),
            P("gx", "gy", None),
            P("gx", "gy", None),
        ),
        out_specs=(P(None, "gx", "gy", None), P(), P(), P()),
        check_vma=False,
    )
```

profile of v0, /device:TPU:14, one launch (start us, length us, event | category | flops | bytes accessed | tf_op | source)
XLA Modules:
  0.0 1131.8 jit_solution(5072555203006667526)
XLA Ops:
  0.6 474.0 %while.31 = (s32[]{:T(128)}, f32[2345,256]{1,0:T(8,128)S(1)}, s32[3,32768]{1,0:T(4,128)}, s32[]{:T(128)}, f32[3,32768]{1,0:T(4,128)}, /*index=5*/s32[]{:T(128)},...) while((s32[]{:T(128)}, f32[2345,256]{1,0:T(8,128)S(1)}, ...), condition=%wide.region_1.2_spmd.clone.clone, body=%wide.region_0.1_spmd.clone.clone.sunk | while | flops 2479059456 | bytes 45443312 | solution.py:85
  10.1 9.3 convert_element_type.169
  20.2 10.1 convolution_add_fusion.2
  39.8 9.3 convert_element_type.169
  49.8 10.1 convolution_add_fusion.2
  69.4 9.3 convert_element_type.169
  79.4 10.1 convolution_add_fusion.2
  99.0 9.3 convert_element_type.169
  109.0 10.1 convolution_add_fusion.2
  128.6 9.3 convert_element_type.169
  138.7 10.1 convolution_add_fusion.2
  158.3 9.3 convert_element_type.169
  168.3 10.1 convolution_add_fusion.2
  187.9 9.3 convert_element_type.169
  197.9 10.1 convolution_add_fusion.2
  217.5 9.3 convert_element_type.169
  227.5 10.1 convolution_add_fusion.2
  247.1 9.3 convert_element_type.169
  257.2 10.1 convolution_add_fusion.2
  276.8 9.3 convert_element_type.169
  286.8 10.1 convolution_add_fusion.2
  306.4 9.3 convert_element_type.169
  316.4 10.1 convolution_add_fusion.2
  336.0 9.3 convert_element_type.169
  346.0 10.1 convolution_add_fusion.2
  365.6 9.3 convert_element_type.169
  375.6 10.1 convolution_add_fusion.2
  395.2 9.3 convert_element_type.169
  405.3 10.1 convolution_add_fusion.2
  424.9 9.3 convert_element_type.169
  434.9 10.1 convolution_add_fusion.2
  454.5 9.3 convert_element_type.169
  464.5 10.1 convolution_add_fusion.2
  505.7 45.7 %all-to-all-done = f32[1,2,256,2048]{3,1,0,2:T(2,128)} async-done(((f32[1,2,256,2048]{3,1,0,2:T(2,128)}), f32[1,2,256,2048]{3,1,0,2:T(2,128)}, u32[]{:S(2)}, u32[]{:S(2)}) %all-to-all-start) | async-done | bytes 4194336 | tf_op jit(solution)/shard_map/all_to_all | solution.py:102
  551.4 8.0 copy.35
  559.4 7.9 reshape.1077
  567.2 17.7 %fusion.64 = f32[2,32,256,64]{2,3,0,1:T(8,128)} fusion(f32[8,2,32,32,64,1]{4,3,0,1,2,5:T(8,128)} %reshape.1077, f32[1,1,256,8,32]{2,4,3,1,0:T(8,128)S(1)} %get-tuple-element.478, f32[1,1,256,8,32]{2,4,3,1,0:T(8,128)S(1)} %get-tuple-element.477, f32[1,1,256,8,32]{2,4,3,1,0:T(8,128)S(1)} %get-tuple-element.476), kind=kOutput, calls=%fused_computation.123 | convolution fusion | flops 6443237376 | bytes 9175040 | tf_op jit(solution)/shard_map/ocKst,scktz->okKz/dot_general | solution.py:105
  584.9 15.2 %copy.26 = f32[2,32,256,64]{1,0,3,2:T(2,128)} copy(f32[2,32,256,64]{2,3,0,1:T(8,128)} %fusion.64) | data formatting | bytes 8388608 | tf_op jit(solution)/shard_map/broadcast_in_dim;reshape | solution.py:107
  600.1 19.4 %reshape.1087 = f32[4,1,262144]{2,1,0:T(1,128)} reshape(f32[16384,1,2,32]{3,2,1,0:T(2,128)} %bitcast.105) | data formatting | bytes 8388608
  627.7 88.8 %all-to-all-done.1 = f32[4,1,262144]{2,1,0:T(1,128)} async-done(((f32[4,1,262144]{2,1,0:T(1,128)}), f32[4,1,262144]{2,1,0:T(1,128)}, u32[]{:S(2)}, u32[]{:S(2)}) %all-to-all-start.1) | async-done | bytes 4194336 | tf_op jit(solution)/shard_map/all_to_all | solution.py:106
  717.0 15.5 %reduce.4 = f32[4,262144]{1,0:T(4,128)} reduce(f32[4,1,262144]{2,1,0:T(1,128)} %all-to-all-done.1, f32[]{:T(128)} %broadcast.1645), dimensions={1}, to_apply=%all_to_all.25.reduce_sub_computation | reduce | bytes 8388612 | tf_op jit(solution)/shard_map/all_to_all | solution.py:106
  732.5 26.8 %reshape.1088 = f32[16384,1,2,32]{3,2,1,0:T(2,128)} reshape(f32[4,262144]{1,0:T(4,128)} %reduce.4) | data formatting | bytes 8388608
  759.3 22.1 %copy.19 = f32[1,2,32,4,4096]{4,3,2,1,0:T(4,128)} copy(f32[1,2,32,4,4096]{2,1,4,3,0:T(2,128)} %bitcast.106) | data formatting | bytes 8388608 | tf_op jit(solution)/shard_map/all_to_all | solution.py:106
  781.3 8.1 reshape.1080
  789.5 9.5 fusion.59
  805.6 222.5 %while.30 = (s32[]{:T(128)}, f32[256]{0:T(256)S(1)}, f32[32,64,256]{2,1,0:T(8,128)}, s32[32,64,256]{2,1,0:T(8,128)}, s32[]{:T(128)}, /*index=5*/s32[]{:T(128)}) while((s32[]{:T(128)}, f32[256]{0:T(256)S(1)}, f32[32,64,256]{2,1,0:T(8,128)}, s32[32,64,256]{2,1,0:T(8,128)}, s32[]{:T(128)}, /*index=5*/s32[]{:T(128)}) %tuple.124), condition=%wide.region_6.7_spmd.clone, body=%wide.region_5.6_spmd.clone.sunk | while | flops 54526464 | bytes 659543 | solution.py:155
  1037.9 45.6 %fusion.82 = f32[3,3]{1,0:T(4,128)S(1)} fusion(f32[1,32,64,256]{3,0,2,1:T(1,128)} %stack_broadcast_in_dim.8, f32[1,32,64,256]{3,0,2,1:T(1,128)} %stack_broadcast_in_dim.7, f32[1,32,64,256]{3,0,2,1:T(1,128)} %stack_broadcast_in_dim.6, f32[32,64,256]{2,1,0:T(8,128)} %get-tuple-element.443, f32[]{:T(128)} %multiply_reduce_fusion), kind=kOutput, calls=%fused_computation.134 | convolution fusion | flops 64487460 | bytes 8388648 | tf_op jit(solution)/shard_map/akyz,bkyz->ab/dot_general | solution.py:142
  1088.4 43.2 %all-reduce = (f32[]{:T(128)}, f32[3,3]{1,0:T(4,128)}, f32[256]{0:T(256)}) all-reduce(f32[]{:T(128)S(6)} %mul.987, f32[3,3]{1,0:T(4,128)S(1)} %fusion.82, f32[256]{0:T(256)S(1)} %broadcast_multiply_fusion.1), channel_id=1, replica_groups=mesh['gx'=8,'gy'=4] {'gx','gy'}, use_global_device_ids=true, to_apply=%region_3.4 | all-reduce | flops 266 | bytes 2128 | tf_op jit(solution)/shard_map/psum | solution.py:157
  (431 shorter events, 443.9 us)
Async XLA Ops:
  474.7 5.4 collective-permute-start
  480.2 5.3 collective-permute-start.1
  498.1 53.2 %all-to-all-start = ((f32[1,2,256,2048]{3,1,0,2:T(2,128)}), f32[1,2,256,2048]{3,1,0,2:T(2,128)}, u32[]{:S(2)}, u32[]{:S(2)}) async-start(f32[1,2,256,2048]{3,1,0,2:T(2,128)} %copy.15), calls=%async_computation | async-start | bytes 8388608 | tf_op jit(solution)/shard_map/all_to_all | solution.py:102
  619.6 96.9 %all-to-all-start.1 = ((f32[4,1,262144]{2,1,0:T(1,128)}), f32[4,1,262144]{2,1,0:T(1,128)}, u32[]{:S(2)}, u32[]{:S(2)}) async-start(f32[4,1,262144]{2,1,0:T(1,128)} %reshape.1087), calls=%async_computation.1 | async-start | bytes 8388608 | tf_op jit(solution)/shard_map/all_to_all | solution.py:106
  799.0 2.1 copy-start
  799.0 3.1 copy-start.2
  804.3 1.4 copy-start.1
where the time goes:
time: 1150 us; the launch traced here: 1130 us
  matrix products  403 us (35%)
  local copies, waits for them, and re-layouts  365 us (32%)
  other arithmetic  163 us (14%)
  waiting for transfers between devices  137 us (12%)
  blocking collectives  43.2 us (4%)
  starting transfers between devices  15.2 us (1%)
    dot_general x32, matrix products, shell_rows(): jnp.dot(power_spectrum_row.reshape(-1), onehot, precision=upper_limit)  163 us
    dot_general x16, matrix products, spread(): jnp.einsum('ap,ax->px', factor_yz, factor_x, preferred_element_type=jnp.f...  162 us
    convert_element_type x16, local copies, waits for them, and re-layouts, spread(): factor_yz = (table_y[:, :, None] * wave_table_z[:, None, :]).reshape(bloc...  148 us
    convert_element_type x16, other arithmetic, spread(): factor_yz = (table_y[:, :, None] * wave_table_z[:, None, :]).reshape(bloc...  113 us
    all_to_all x1, waiting for transfers between devices, shards(): lax.all_to_all(along_y.reshape(2, kx_rows, MESH * keep_z)[None], 'gy', sp...  88.8 us
    while x128, local copies, waits for them, and re-layouts  57.7 us
    unnamed x8, local copies, waits for them, and re-layouts  49 us
    all_to_all x1, waiting for transfers between devices, shards(): lax.all_to_all(along_x[None], 'gx', split_axis=2, concat_axis=0, tiled=True)  45.7 us
  transfers between devices with their start and end apart: 4, of which 4 were waited for; matrix products, arithmetic and copies ran while one was open for 1% of the time, Pallas kernels for 0%

commit v1 on v0

--- a/solution.py
+++ b/solution.py
@@ -103,13 +103,11 @@
     moved = moved.reshape(rows_y, 2, kx_rows, keep_y, keep_z)
     table_y = complex_table.reshape(2, 2, MESH, rows_y, plane_y)
     along_y = jnp.einsum("ocKst,scktz->okKz", table_y, moved, precision=upper_limit)
-    shifted_along_z = lax.all_to_all(
-        along_y.reshape(2, kx_rows, MESH * keep_z)[None],
-        "gy",
-        split_axis=3,
-        concat_axis=0,
-        tiled=True,
-    )
+    x = along_y.reshape(2, kx_rows, MESH * keep_z)[None]
+    count_2 = lax.axis_size("gy")
+    parts = jnp.stack(jnp.split(x, count_2, axis=3), axis=0)
+    parts = lax.all_to_all(parts, "gy", split_axis=0, concat_axis=0)
+    shifted_along_z = jnp.concatenate(parts, axis=0)
     shifted_along_z = shifted_along_z.reshape(cols_z, 2, kx_rows, ky_rows, keep_z)
     wave_table_z = complex_table.reshape(2, 2, MESH, cols_z, plane_z)
     structure_factor = jnp.einsum(

time: 1150 us -> 1040 us (0.904)
  local copies, waits for them, and re-layouts: 365 us -> 280 us
  other arithmetic: 163 us -> 148 us
    unnamed x8 -> x5, local copies, waits for them, and re-layouts: 49 us -> 4.71 us
    while x128, local copies, waits for them, and re-layouts: 57.7 us -> 30.9 us
    all_to_all x2 -> x1, local copies, waits for them, and re-layouts: 22.6 us -> 6.9 us  [shards(): parts = lax.all_to_all(parts, 'gy', split_axis=0, concat_axis=0)]
    all_to_all x1 -> x0, other arithmetic: 15.5 us -> none  [shards(): lax.all_to_all(along_y.reshape(2, kx_rows, MESH * keep_z)[None], 'gy', sp...]
where the time goes in v1:
time: 1040 us; the launch traced here: 1030 us
  matrix products  403 us (39%)
  local copies, waits for them, and re-layouts  280 us (27%)
  other arithmetic  148 us (14%)
  waiting for transfers between devices  137 us (13%)
  blocking collectives  43.2 us (4%)
  starting transfers between devices  14.8 us (1%)
    dot_general x32, matrix products, shell_rows(): jnp.dot(power_spectrum_row.reshape(-1), onehot, precision=upper_limit)  163 us
    dot_general x16, matrix products, spread(): jnp.einsum('ap,ax->px', factor_yz, factor_x, preferred_element_type=jnp.f...  162 us
    convert_element_type x16, local copies, waits for them, and re-layouts, spread(): factor_yz = (table_y[:, :, None] * wave_table_z[:, None, :]).reshape(bloc...  149 us
    convert_element_type x16, other arithmetic, spread(): factor_yz = (table_y[:, :, None] * wave_table_z[:, None, :]).reshape(bloc...  113 us
    all_to_all x1, waiting for transfers between devices, shards(): parts = lax.all_to_all(parts, 'gy', split_axis=0, concat_axis=0)  88.8 us
    all_to_all x1, waiting for transfers between devices, shards(): lax.all_to_all(along_x[None], 'gx', split_axis=2, concat_axis=0, tiled=True)  45.7 us
    dot_general x1, matrix products, shards(): jnp.einsum('akyz,bkyz->ab', vectors * coef[None], vectors, precision=uppe...  45.5 us
    psum x1, blocking collectives, shards(): lax.psum((energy_part, virial_part, spectrum_part), ('gx', 'gy'))  43.2 us
  transfers between devices with their start and end apart: 4, of which 4 were waited for; matrix products, arithmetic and copies ran while one was open for 1% of the time, Pallas kernels for 0%

profile of v1, /device:TPU:14, one launch (start us, length us, event | category | flops | bytes accessed | tf_op | source)
XLA Modules:
  0.0 1030.8 jit_solution(5828784399566122841)
XLA Ops:
  0.6 474.1 %while.31 = (s32[]{:T(128)}, f32[2345,256]{1,0:T(8,128)S(1)}, s32[3,32768]{1,0:T(4,128)}, s32[]{:T(128)}, f32[3,32768]{1,0:T(4,128)}, /*index=5*/s32[]{:T(128)},...) while((s32[]{:T(128)}, f32[2345,256]{1,0:T(8,128)S(1)}, ...), condition=%wide.region_1.2_spmd.clone.clone, body=%wide.region_0.1_spmd.clone.clone.sunk | while | flops 2479059456 | bytes 45443312 | solution.py:85
  3.1 7.1 multiply_convert_fusion.6
  10.1 9.3 convert_element_type.169
  20.2 10.1 convolution_add_fusion.2
  32.7 7.1 multiply_convert_fusion.6
  39.8 9.3 convert_element_type.169
  49.8 10.1 convolution_add_fusion.2
  69.4 9.3 convert_element_type.169
  79.4 10.1 convolution_add_fusion.2
  91.9 7.1 multiply_convert_fusion.6
  99.0 9.3 convert_element_type.169
  109.1 10.1 convolution_add_fusion.2
  121.6 7.1 multiply_convert_fusion.6
  128.7 9.3 convert_element_type.169
  138.7 10.1 convolution_add_fusion.2
  158.3 9.3 convert_element_type.169
  168.3 10.1 convolution_add_fusion.2
  187.9 9.3 convert_element_type.169
  198.0 10.1 convolution_add_fusion.2
  217.6 9.3 convert_element_type.169
  227.6 10.1 convolution_add_fusion.2
  247.2 9.3 convert_element_type.169
  257.2 10.1 convolution_add_fusion.2
  276.8 9.3 convert_element_type.169
  286.9 10.1 convolution_add_fusion.2
  306.5 9.3 convert_element_type.169
  316.5 10.1 convolution_add_fusion.2
  336.1 9.3 convert_element_type.169
  346.1 10.1 convolution_add_fusion.2
  365.7 9.3 convert_element_type.169
  375.8 10.1 convolution_add_fusion.2
  395.4 9.3 convert_element_type.169
  405.4 10.1 convolution_add_fusion.2
  425.0 9.3 convert_element_type.169
  435.0 10.1 convolution_add_fusion.2
  454.6 9.3 convert_element_type.169
  464.7 10.1 convolution_add_fusion.2
  505.5 45.7 %all-to-all-done = f32[1,2,256,2048]{3,1,0,2:T(2,128)} async-done(((f32[1,2,256,2048]{3,1,0,2:T(2,128)}), f32[1,2,256,2048]{3,1,0,2:T(2,128)}, u32[]{:S(2)}, u32[]{:S(2)}) %all-to-all-start) | async-done | bytes 4194336 | tf_op jit(solution)/shard_map/all_to_all | solution.py:102
  551.1 8.0 copy.31
  559.1 7.9 reshape.1072
  567.0 17.7 %fusion.64 = f32[2,32,256,64]{2,3,0,1:T(8,128)} fusion(f32[8,2,32,32,64,1]{4,3,0,1,2,5:T(8,128)} %reshape.1072, f32[1,1,256,8,32]{2,4,3,1,0:T(8,128)S(1)} %get-tuple-element.486, f32[1,1,256,8,32]{2,4,3,1,0:T(8,128)S(1)} %get-tuple-element.485, f32[1,1,256,8,32]{2,4,3,1,0:T(8,128)S(1)} %get-tuple-element.484), kind=kOutput, calls=%fused_computation.123 | convolution fusion | flops 6443237376 | bytes 9175040 | tf_op jit(solution)/shard_map/ocKst,scktz->okKz/dot_general | solution.py:105
  591.6 7.3 broadcast_in_dim_reshape.3
  611.7 88.8 %all-to-all-done.1 = f32[4,1,2,32,4096]{4,3,2,1,0:T(8,128)} async-done(((f32[4,1,2,32,4096]{4,3,2,1,0:T(8,128)}), f32[4,1,2,32,4096]{4,3,2,1,0:T(8,128)}, u32[]{:S(2)}, u32[]{:S(2)}) %all-to-all-start.1) | async-done | bytes 4194336 | tf_op jit(solution)/shard_map/all_to_all | solution.py:109
  707.4 8.2 reshape.1075
  715.6 9.8 fusion.67
  731.3 196.1 %while.30 = (s32[]{:T(128)}, f32[256]{0:T(256)S(1)}, f32[32,64,256]{2,1,0:T(8,128)S(1)}, s32[32,64,256]{2,1,0:T(8,128)}, s32[]{:T(128)}, /*index=5*/s32[]{:T(128)}) while((s32[]{:T(128)}, f32[256]{0:T(256)S(1)}, f32[32,64,256]{2,1,0:T(8,128)S(1)}, s32[32,64,256]{2,1,0:T(8,128)}, s32[]{:T(128)}, /*index=5*/s32[]{:T(128)}) %tuple.125), condition=%wide.region_6.7_spmd.clone, body=%wide.region_5.6_spmd.clone.sunk | while | flops 54526464 | bytes 659543 | solution.py:153
  937.2 45.5 %fusion.85 = f32[3,3]{1,0:T(4,128)S(1)} fusion(f32[1,32,64,256]{3,0,2,1:T(1,128)} %stack_broadcast_in_dim.8, f32[1,32,64,256]{3,0,2,1:T(1,128)} %stack_broadcast_in_dim.7, f32[1,32,64,256]{3,0,2,1:T(1,128)} %stack_broadcast_in_dim.6, f32[32,64,256]{2,1,0:T(8,128)S(1)} %copy-done.1, f32[]{:T(128)} %multiply_reduce_fusion), kind=kOutput, calls=%fused_computation.135 | convolution fusion | flops 64487460 | bytes 8388648 | tf_op jit(solution)/shard_map/akyz,bkyz->ab/dot_general | solution.py:140
  987.4 43.2 %all-reduce = (f32[]{:T(128)}, f32[3,3]{1,0:T(4,128)}, f32[256]{0:T(256)}) all-reduce(f32[]{:T(128)S(6)} %mul.987, f32[3,3]{1,0:T(4,128)S(1)} %fusion.85, f32[256]{0:T(256)S(1)} %broadcast_multiply_fusion.1), channel_id=1, replica_groups=mesh['gx'=8,'gy'=4] {'gx','gy'}, use_global_device_ids=true, to_apply=%region_3.4 | all-reduce | flops 266 | bytes 2128 | tf_op jit(solution)/shard_map/psum | solution.py:155
  (428 shorter events, 405.7 us)
Async XLA Ops:
  474.9 5.4 collective-permute-start
  480.3 5.2 collective-permute-start.1
  498.2 53.0 %all-to-all-start = ((f32[1,2,256,2048]{3,1,0,2:T(2,128)}), f32[1,2,256,2048]{3,1,0,2:T(2,128)}, u32[]{:S(2)}, u32[]{:S(2)}) async-start(f32[1,2,256,2048]{3,1,0,2:T(2,128)} %copy.18), calls=%async_computation | async-start | bytes 8388608 | tf_op jit(solution)/shard_map/all_to_all | solution.py:102
  603.6 96.9 %all-to-all-start.1 = ((f32[4,1,2,32,4096]{4,3,2,1,0:T(8,128)}), f32[4,1,2,32,4096]{4,3,2,1,0:T(8,128)}, u32[]{:S(2)}, u32[]{:S(2)}) async-start(f32[4,1,2,32,4096]{4,3,2,1,0:T(8,128)} %pad_maximum_fusion), calls=%async_computation.1 | async-start | bytes 8388608 | tf_op jit(solution)/shard_map/all_to_all | solution.py:109
  715.6 9.8 copy-start
  930.7 6.6 copy-start.1
